TPU v7x, 256 devices: a whole 4x4x8 slice. The times are simulated.
256 devices in a mesh: chan: 2 (over y_hi), seq: 16 (over z, core), dp: 8 (over x, y_lo).
Axes of the slice: x: 4, y: 4 (y_hi: 2, y_lo: 2; y = y_hi * 2 + y_lo), z: 8, core: 2. Of those that a mesh axis runs over, the one named last changes fastest.
Arguments:
- queries: bfloat16 [8, 2, 2048, 2048], P('dp', 'chan', 'seq'), may hold values from -8 to 8
- keys: bfloat16 [8, 2, 2048, 2048], P('dp', 'chan', 'seq'), may hold values from -8 to 8
- values: bfloat16 [8, 2, 2048, 2048], P('dp', 'chan', 'seq'), may hold values from -6 to 6
- out_grad: bfloat16 [8, 2, 2048, 2048], P('dp', 'chan', 'seq'), may hold values from -6 to 6
- cross_bias: float32 [16], replicated, may hold values from -2 to 2
- lengths: int32 [8], P('dp'), may hold values from 512 to 2048
Outputs:
- query_grad: bfloat16 [8, 2, 2048, 2048], P('dp', 'chan', 'seq')
- key_grad: bfloat16 [8, 2, 2048, 2048], P('dp', 'chan', 'seq')
- value_grad: bfloat16 [8, 2, 2048, 2048], P('dp', 'chan', 'seq')
- bias_grad: float32 [16], replicated
Inputs may be any that keep to these rules, and one draw needn't show every extreme that they name: Frames of conversation b from lengths[b] on are padding in both channels.
All inputs are finite; a program needn't handle non-finite values.
Results may differ from a plain program's by a relative error of at most 0.011.
Values may be sent and summed in bfloat16 or wider, within the bound.
A program may use at most 128 MiB of HBM per device.

v0:
```python
import functools
import math

import jax
import jax.numpy as jnp
from jax import lax
from jax.sharding import Mesh
from jax.sharding import PartitionSpec as P

LOOKBACK = 6
SEQ = ("seq_0", "seq_1")
CHAN_SEQ_DP = ("chan", "seq_0", "seq_1", "dp_0", "dp_1")
DP = ("dp_0", "dp_1")


NEG_FILL = -1e30


def swapped(value, axis, apart):
    mask = 2**apart
    pairs = [(source, source ^ mask) for source in range(lax.axis_size(axis))]
    return lax.ppermute(value, axis, pairs)


def from_behind(value, axis, steps):
    count = lax.axis_size(axis)
    first, last = (max(0, -steps), min(count, count - steps))
    return lax.ppermute(value, axis, [(source, source + steps) for source in range(first, last)])


def from_everyone(array, axis):
    size = lax.axis_size(axis)
    return lax.all_to_all(
        jnp.broadcast_to(array[None], (size, *array.shape)), axis, 0, 0, tiled=True
    )


def of_everyone(array, axis):
    everything = from_everyone(array, axis)
    return jnp.max(everything, axis=0)


def of_everyone_2(array, axis):
    return from_everyone(array, axis).sum(axis=0)


def in_one(arrays, axis):
    ends = [0]
    for a in arrays:
        ends.append(ends[-1] + a.size)
    total = of_everyone_2(jnp.concatenate([a.ravel() for a in arrays]), axis)
    return tuple((total[b:e].reshape(a.shape) for a, b, e in zip(arrays, ends, ends[1:])))


def by_axis(array, axes):
    return functools.reduce(lax.psum, axes, array)


def local_scores(query_part, key_part, bias_part, allowed, root_scale):
    scores = jnp.einsum("pgd,sgd->gps", query_part, key_part, preferred_element_type=jnp.float32)
    scores = scores * root_scale + bias_part
    return jnp.where(allowed[None], scores, NEG_FILL)


def forward_stats(query_heads, grad_heads, key_heads, value_heads, bias_heads, allowed, root_scale):
    row_count, head_count, head_width = query_heads.shape

    def forward_group_step(head_group, carried):
        row_max, row_total, row_moment = carried
        offset = head_group * 2
        query_part = lax.dynamic_slice_in_dim(query_heads, offset, 2, 1)
        grad_part = lax.dynamic_slice_in_dim(grad_heads, offset, 2, 1)
        key_part = lax.dynamic_slice_in_dim(key_heads, offset, 2, 1)
        value_part = lax.dynamic_slice_in_dim(value_heads, offset, 2, 1)
        bias_part = lax.dynamic_slice_in_dim(bias_heads, offset, 2, 0)[:, :, None]
        scores = local_scores(query_part, key_part, bias_part, allowed, root_scale)
        group_max = jnp.max(scores, axis=2)
        weights = jnp.where(allowed[None], jnp.exp(scores - group_max[:, :, None]), 0.0)
        weight_grad = jnp.einsum(
            "pgd,sgd->gps", grad_part, value_part, preferred_element_type=jnp.float32
        )
        group_total = jnp.sum(weights, axis=2)
        group_moment = jnp.sum(weights * weight_grad, axis=2)
        row_max = lax.dynamic_update_slice_in_dim(row_max, group_max, offset, 0)
        row_total = lax.dynamic_update_slice_in_dim(row_total, group_total, offset, 0)
        row_moment = lax.dynamic_update_slice_in_dim(row_moment, group_moment, offset, 0)
        return (row_max, row_total, row_moment)

    initial = (
        jnp.zeros((head_count, row_count), jnp.float32),
        jnp.zeros((head_count, row_count), jnp.float32),
        jnp.zeros((head_count, row_count), jnp.float32),
    )
    return lax.fori_loop(0, head_count // 2, forward_group_step, initial)


def backward_local(
    query_heads,
    grad_heads,
    key_heads,
    value_heads,
    bias_heads,
    partner_flag,
    allowed,
    log_norm,
    row_delta,
    root_scale,
):
    row_count, head_count, head_width = query_heads.shape
    key_count = key_heads.shape[0]

    def backward_group_step(head_group, carried):
        query_sum, key_sum, value_sum, bias_sum = carried
        offset = head_group * 2
        query_part = lax.dynamic_slice_in_dim(query_heads, offset, 2, 1)
        grad_part = lax.dynamic_slice_in_dim(grad_heads, offset, 2, 1)
        key_part = lax.dynamic_slice_in_dim(key_heads, offset, 2, 1)
        value_part = lax.dynamic_slice_in_dim(value_heads, offset, 2, 1)
        bias_part = lax.dynamic_slice_in_dim(bias_heads, offset, 2, 0)[:, :, None]
        norm_part = lax.dynamic_slice_in_dim(log_norm, offset, 2, 0)[:, :, None]
        delta_part = lax.dynamic_slice_in_dim(row_delta, offset, 2, 0)[:, :, None]
        scores = local_scores(query_part, key_part, bias_part, allowed, root_scale)
        weights = jnp.where(allowed[None], jnp.exp(scores - norm_part), 0.0)
        weight_grad = jnp.einsum(
            "pgd,sgd->gps", grad_part, value_part, preferred_element_type=jnp.float32
        )
        score_grad = weights * (weight_grad - delta_part)
        weight_low = weights.astype(jnp.bfloat16)
        score_low = score_grad.astype(jnp.bfloat16)
        query_term = (
            jnp.einsum("gps,sgd->pgd", score_low, key_part, preferred_element_type=jnp.float32)
            * root_scale
        )
        key_term = (
            jnp.einsum("gps,pgd->sgd", score_low, query_part, preferred_element_type=jnp.float32)
            * root_scale
        )
        value_term = jnp.einsum(
            "gps,pgd->sgd", weight_low, grad_part, preferred_element_type=jnp.float32
        )
        bias_term = jnp.sum(score_grad * partner_flag[None, :, None], axis=(1, 2))
        query_sum = lax.dynamic_update_slice_in_dim(query_sum, query_term, offset, 1)
        key_sum = lax.dynamic_update_slice_in_dim(key_sum, key_term, offset, 1)
        value_sum = lax.dynamic_update_slice_in_dim(value_sum, value_term, offset, 1)
        bias_sum = lax.dynamic_update_slice_in_dim(bias_sum, bias_term, offset, 0)
        return (query_sum, key_sum, value_sum, bias_sum)

    initial = (
        jnp.zeros((row_count, head_count, head_width), jnp.float32),
        jnp.zeros((key_count, head_count, head_width), jnp.float32),
        jnp.zeros((key_count, head_count, head_width), jnp.float32),
        jnp.zeros((head_count,), jnp.float32),
    )
    return lax.fori_loop(0, head_count // 2, backward_group_step, initial)


def shards(queries, keys, values, out_grad, cross_bias, lengths):
    frames = queries.shape[2]
    feature_width = queries.shape[3]
    head_count = cross_bias.shape[0]
    head_width = feature_width // head_count
    root_scale = 1.0 / math.sqrt(head_width)
    channel = lax.axis_index("chan")
    block_index = lax.axis_index(SEQ)
    dialog_length = lengths[0]
    own_query = queries[0, 0]
    own_grad = out_grad[0, 0]
    own_keys = keys[0, 0]
    own_values = values[0, 0]
    partner_query, partner_grad = swapped((own_query, own_grad), "chan", 0)
    leading = channel == 0
    query_rows = jnp.where(
        leading,
        jnp.concatenate([own_query, partner_query], axis=0),
        jnp.concatenate([partner_query, own_query], axis=0),
    )
    grad_rows = jnp.where(
        leading,
        jnp.concatenate([own_grad, partner_grad], axis=0),
        jnp.concatenate([partner_grad, own_grad], axis=0),
    )
    tower_index = jnp.arange(2 * frames, dtype=jnp.int32) // frames
    partner_flag = (tower_index != channel).astype(jnp.float32)
    pieces = [None] * LOOKBACK + [(own_keys, own_values)]
    moving = (own_keys, own_values)
    for distance in range(1, LOOKBACK + 1):
        moving = from_behind((moving[0], moving[1]), SEQ, 1)
        pieces[LOOKBACK - distance] = moving
    key_window = jnp.concatenate([shard_pair[0] for shard_pair in pieces], axis=0)
    value_window = jnp.concatenate([shard_pair[1] for shard_pair in pieces], axis=0)
    window_rows = key_window.shape[0]
    reach_frames = LOOKBACK * frames
    own_frames = block_index * frames + jnp.arange(frames, dtype=jnp.int32)
    query_frame = jnp.concatenate([own_frames, own_frames])
    key_frame = (block_index - LOOKBACK) * frames + jnp.arange(window_rows, dtype=jnp.int32)
    allowed = (key_frame[None, :] > query_frame[:, None] - reach_frames) & (
        key_frame[None, :] <= query_frame[:, None]
    )
    allowed = allowed & (key_frame[None, :] >= 0) & (key_frame[None, :] < dialog_length)
    allowed = allowed & (query_frame[:, None] < dialog_length)
    query_heads = query_rows.reshape(2 * frames, head_count, head_width)
    grad_heads = grad_rows.reshape(2 * frames, head_count, head_width)
    key_heads = key_window.reshape(window_rows, head_count, head_width)
    value_heads = value_window.reshape(window_rows, head_count, head_width)
    bias_heads = cross_bias[:, None] * partner_flag[None, :]
    row_max, row_total, row_moment = forward_stats(
        query_heads, grad_heads, key_heads, value_heads, bias_heads, allowed, root_scale
    )
    merged_peak = of_everyone(row_max, "chan")
    rescale = jnp.exp(row_max - merged_peak)
    merged_total, merged_moment = in_one((row_total * rescale, row_moment * rescale), "chan")
    safe_total = jnp.where(merged_total > 0.0, merged_total, 1.0)
    log_norm = merged_peak + jnp.log(safe_total)
    row_delta = merged_moment / safe_total
    query_sum, key_sum, value_sum, bias_sum = backward_local(
        query_heads,
        grad_heads,
        key_heads,
        value_heads,
        bias_heads,
        partner_flag,
        allowed,
        log_norm,
        row_delta,
        root_scale,
    )
    query_flat = query_sum.reshape(2 * frames, feature_width)
    own_part = jnp.where(leading, query_flat[:frames], query_flat[frames:])
    other_part = jnp.where(leading, query_flat[frames:], query_flat[:frames])
    arrived_query = swapped(other_part.astype(jnp.bfloat16), "chan", 0).astype(other_part.dtype)
    query_out = (own_part + arrived_query).astype(jnp.bfloat16)
    key_flat = key_sum.reshape(window_rows, feature_width)
    value_flat = value_sum.reshape(window_rows, feature_width)

    def key_block(position):
        return key_flat[position * frames : (position + 1) * frames]

    def value_block(position):
        return value_flat[position * frames : (position + 1) * frames]

    running = (key_block(0), value_block(0))
    for distance in range(1, LOOKBACK + 1):
        arrived = (
            from_behind(running[0].astype(jnp.bfloat16), SEQ, -1).astype(jnp.float32),
            from_behind(running[1].astype(jnp.bfloat16), SEQ, -1).astype(jnp.float32),
        )
        running = (arrived[0] + key_block(distance), arrived[1] + value_block(distance))
    bias_out = by_axis(bias_sum, CHAN_SEQ_DP)
    return (
        query_out[None, None],
        running[0].astype(jnp.bfloat16)[None, None],
        running[1].astype(jnp.bfloat16)[None, None],
        bias_out,
    )


def solution(mesh):
    torus = Mesh(
        mesh.devices.reshape(mesh.shape["chan"], 8, 2, 4, 2),
        ("chan", "seq_0", "seq_1", "dp_0", "dp_1"),
    )
    in_specs = (
        P(DP, "chan", SEQ, None),
        P(DP, "chan", SEQ, None),
        P(DP, "chan", SEQ, None),
        P(DP, "chan", SEQ, None),
        P(),
        P(DP),
    )
    out_specs = (P(DP, "chan", SEQ, None), P(DP, "chan", SEQ, None), P(DP, "chan", SEQ, None), P())
    return jax.shard_map(
        shards, mesh=torus, in_specs=in_specs, out_specs=out_specs, check_vma=False
    )
```

profile of v0, /device:TPU:32, one launch (start us, length us, event | category | flops | bytes accessed | tf_op | source)
XLA Modules:
  0.0 416.2 jit_solution(15948245657260820037)
XLA Ops:
  5.2 3.9 collective-permute-start.8
  9.1 3.3 collective-permute-done
  14.4 3.7 collective-permute-done.8
  20.0 3.7 collective-permute-done.1
  25.6 3.7 collective-permute-done.9
  31.2 3.8 collective-permute-done.2
  38.3 3.3 collective-permute-start.7
  44.0 3.4 collective-permute-start.11
  47.4 2.5 collective-permute-start.4
  49.9 4.9 %collective-permute-done.11 = bf16[128,2048]{0,1:T(8,128)(2,1)} collective-permute-done((bf16[128,2048]{0,1:T(8,128)(2,1)}, bf16[128,2048]{0,1:T(8,128)(2,1)}, u32[]{:S(2)}, u32[]{:S(2)}) %collective-permute-start.11) | collective-permute-done | bytes 524320 | tf_op jit(solution)/shard_map/ppermute | solution.py:28
  56.7 3.7 collective-permute-done.4
  69.2 3.9 collective-permute-start.13
  83.6 6.0 %copy.115 = bf16[896,16,128]{2,0,1:T(8,128)(2,1)} copy(bf16[896,16,128]{0,2,1:T(8,128)(2,1)} %constant_dynamic-update-slice_fusion.3) | data formatting | bytes 7340032
  99.1 6.0 %copy.113 = bf16[896,16,128]{2,0,1:T(8,128)(2,1)} copy(bf16[896,16,128]{0,2,1:T(8,128)(2,1)} %constant_dynamic-update-slice_fusion.10) | data formatting | bytes 7340032
  105.1 37.3 %while.38 = (s32[]{:T(128)}, f32[16,256]{1,0:T(8,128)S(1)}, f32[16,256]{1,0:T(8,128)S(1)}, f32[16,256]{1,0:T(8,128)S(1)}, bf16[256,16,128]{2,0,1:T(8,128)(2,1)},...) while((s32[]{:T(128)}, f32[16,256]{1,0:T(8,128)S(1)}, ...), condition=%wide.region_4.5_spmd.clone, body=%wide.region_0.4_spmd.clone.sunk | while | flops 241302016 | bytes 7640807 | solution.py:94
  142.4 9.8 %all_to_all.11 = f32[2,16,256]{2,1,0:T(8,128)S(1)} all-to-all(f32[2,16,256]{2,1,0:T(8,128)S(1)} %broadcast_in_dim.128), channel_id=1, replica_groups=mesh['chan'=2,'seq_0'=8,'seq_1'=2,'dp_0'=4,'dp_1'=2] {'chan'}, dimensions={0} | all-to-all | bytes 65536 | tf_op jit(solution)/shard_map/all_to_all | solution.py:33
  152.9 3.5 all-to-all-start.1
  156.4 5.4 %all-to-all-done.1 = f32[2,1,8192]{2,1,0:T(1,128)S(1)} async-done(((f32[2,1,8192]{2,1,0:T(1,128)}), f32[2,1,8192]{2,1,0:T(1,128)S(1)}, u32[]{:S(2)}, u32[]{:S(2)}) %all-to-all-start.1) | async-done | bytes 65568 | tf_op jit(solution)/shard_map/all_to_all | solution.py:33
  163.6 3.8 broadcast.133.clone
  167.4 3.7 broadcast.133
  171.1 85.7 %while.39 = (s32[]{:T(128)}, f32[256,16,128]{0,2,1:T(8,128)}, f32[896,16,128]{0,2,1:T(8,128)}, f32[896,16,128]{0,2,1:T(8,128)}, f32[16]{0:T(128)S(1)}, /*index=5...) while((s32[]{:T(128)}, f32[256,16,128]{0,2,1:T(8,128)}, ...), condition=%wide.region_9.10_spmd.clone, body=%wide.region_7.9_spmd.clone.sunk | while | flops 593922560 | bytes 12747555 | solution.py:154
  188.1 2.3 fusion.74
  261.0 5.2 %fusion.41 = (f32[128,16,128]{0,2,1:T(8,128)}, f32[128,16,128]{0,2,1:T(8,128)}, f32[128,16,128]{0,2,1:T(8,128)}, f32[128,16,128]{0,2,1:T(8,128)}, f32[128,16,128]{0,2,1:T(8,128)S(1)}, /*index=5*/f32[128,16,128]{0,2,1:T(8,128)S(1)}) fusion(f32[896,16,128]{0,2,1:T(8,128)} %get-tuple-element.411), kind=kLoop, calls=%fused_computation.111 | loop fusion | bytes 12582912 | tf_op jit(solution)/shard_map/slice | solution.py:236
  270.7 5.3 %fusion.40 = (f32[128,16,128]{0,2,1:T(8,128)}, f32[128,16,128]{0,2,1:T(8,128)}, f32[128,16,128]{0,2,1:T(8,128)}, f32[128,16,128]{0,2,1:T(8,128)S(1)}, f32[128,16,128]{0,2,1:T(8,128)}, /*index=5*/f32[128,16,128]{0,2,1:T(8,128)}) fusion(f32[896,16,128]{0,2,1:T(8,128)} %get-tuple-element.412), kind=kLoop, calls=%fused_computation.110 | loop fusion | bytes 12582912 | tf_op jit(solution)/shard_map/slice | solution.py:239
  275.9 2.5 copy.141
  278.5 2.5 copy.148
  281.0 2.3 add_convert_fusion.5
  285.2 2.3 add_convert_fusion.11
  289.4 2.6 copy.149
  293.3 2.3 add_convert_fusion.4
  295.5 2.7 collective-permute-start.23
  298.3 2.3 add_convert_fusion.10
  300.5 3.3 collective-permute-start.17
  305.2 2.7 copy.143
  312.1 2.3 add_convert_fusion.9
  314.4 2.6 collective-permute-start.18
  318.1 2.5 copy.151
  320.6 2.5 copy.144
  327.3 2.3 add_convert_fusion.8
  336.1 2.6 copy.145
  338.7 2.5 copy.152
  343.1 14.0 %psum.35 = f32[16]{0:T(128)S(1)} all-reduce(f32[16]{0:T(128)S(1)} %get-tuple-element.413), channel_id=1, replica_groups=mesh['chan'=2,'seq_0'=8,'seq_1'=2,'dp_0'=4,'dp_1'=2] {'chan'}, use_global_device_ids=true, to_apply=%region_10.11 | all-reduce | flops 16 | bytes 128 | tf_op jit(solution)/shard_map/psum | solution.py:56
  357.1 24.1 %psum.36 = f32[16]{0:T(128)S(1)} all-reduce(f32[16]{0:T(128)S(1)} %psum.35), channel_id=1, replica_groups=mesh['chan'=2,'seq_0'=8,'seq_1'=2,'dp_0'=4,'dp_1'=2] {'seq_0'}, use_global_device_ids=true, to_apply=%region_11.12 | all-reduce | flops 16 | bytes 128 | tf_op jit(solution)/shard_map/psum | solution.py:56
  381.2 2.5 psum.37
  383.6 10.4 %psum.38 = f32[16]{0:T(128)S(1)} all-reduce(f32[16]{0:T(128)S(1)} %psum.37), channel_id=1, replica_groups=mesh['chan'=2,'seq_0'=8,'seq_1'=2,'dp_0'=4,'dp_1'=2] {'dp_0'}, use_global_device_ids=true, to_apply=%region_13.14 | all-reduce | flops 16 | bytes 128 | tf_op jit(solution)/shard_map/psum | solution.py:56
  394.0 5.4 %psum.39 = f32[16]{0:T(128)} all-reduce(f32[16]{0:T(128)S(1)} %psum.38), channel_id=1, replica_groups=mesh['chan'=2,'seq_0'=8,'seq_1'=2,'dp_0'=4,'dp_1'=2] {'dp_1'}, use_global_device_ids=true, to_apply=%region_14.15 | all-reduce | flops 16 | bytes 128 | tf_op jit(solution)/shard_map/psum | solution.py:56
  404.3 4.3 %collective-permute-start.20 = (bf16[128,2048]{1,0:T(8,128)(2,1)S(1)}, bf16[128,2048]{1,0:T(8,128)(2,1)S(1)}, u32[]{:S(2)}, u32[]{:S(2)}) collective-permute-start(bf16[128,2048]{1,0:T(8,128)(2,1)S(1)} %add_convert_fusion.7), channel_id=1, source_target_pairs={{8,0},{16,8},{24,16},{32,24},{40,32},{48,40},{56,48},{64,56},{72,6... | collective-permute-start | bytes 1572872 | tf_op jit(solution)/shard_map/ppermute | solution.py:28
  411.5 3.8 collective-permute-done.20
  (263 shorter events, 211.7 us)
Async XLA Ops:
  0.6 61.7 %copy-start.12 = (f32[16]{0:T(128)S(1)}, f32[16]{0:T(128)}, u32[]{:S(2)}) copy-start(f32[16]{0:T(128)} %param.14) | copy-start | bytes 196
  2.0 10.5 %collective-permute-start = (bf16[128,2048]{0,1:T(8,128)(2,1)S(1)}, bf16[128,2048]{0,1:T(8,128)(2,1)S(1)}, u32[]{:S(2)}, u32[]{:S(2)}) collective-permute-start(bf16[128,2048]{0,1:T(8,128)(2,1)S(1)} %bitcast.96), channel_id=1, source_target_pairs={{0,8},{8,16},{16,24},{24,32},{32,40},{40,48},{48,56},{56,64},{64,7... | collective-permute-start | bytes 1572872 | tf_op jit(solution)/shard_map/ppermute | solution.py:28
  5.2 12.9 %collective-permute-start.8 = (bf16[128,2048]{0,1:T(8,128)(2,1)S(1)}, bf16[128,2048]{0,1:T(8,128)(2,1)S(1)}, u32[]{:S(2)}, u32[]{:S(2)}) collective-permute-start(bf16[128,2048]{0,1:T(8,128)(2,1)S(1)} %bitcast.94), channel_id=1, source_target_pairs={{0,8},{8,16},{16,24},{24,32},{32,40},{40,48},{48,56},{56,64},{64,7... | collective-permute-start | bytes 1572872 | tf_op jit(solution)/shard_map/ppermute | solution.py:28
  12.5 25.8 %copy-start.8 = (bf16[128,2048]{0,1:T(8,128)(2,1)}, bf16[128,2048]{0,1:T(8,128)(2,1)S(1)}, u32[]{:S(2)}) copy-start(bf16[128,2048]{0,1:T(8,128)(2,1)S(1)} %collective-permute-done) | copy-start | bytes 1572868
  12.5 11.2 %collective-permute-start.1 = (bf16[128,2048]{0,1:T(8,128)(2,1)S(1)}, bf16[128,2048]{0,1:T(8,128)(2,1)S(1)}, u32[]{:S(2)}, u32[]{:S(2)}) collective-permute-start(bf16[128,2048]{0,1:T(8,128)(2,1)S(1)} %collective-permute-done), channel_id=1, source_target_pairs={{0,8},{8,16},{16,24},{24,32},{32,40},{40,48},{48,56},{56,64},{64,7... | collective-permute-start | bytes 1572872 | tf_op jit(solution)/shard_map/ppermute | solution.py:28
  18.1 17.0 %copy-start.4 = (bf16[128,2048]{0,1:T(8,128)(2,1)}, bf16[128,2048]{0,1:T(8,128)(2,1)S(1)}, u32[]{:S(2)}) copy-start(bf16[128,2048]{0,1:T(8,128)(2,1)S(1)} %collective-permute-done.8) | copy-start | bytes 1572868
  18.1 11.2 %collective-permute-start.9 = (bf16[128,2048]{0,1:T(8,128)(2,1)S(1)}, bf16[128,2048]{0,1:T(8,128)(2,1)S(1)}, u32[]{:S(2)}, u32[]{:S(2)}) collective-permute-start(bf16[128,2048]{0,1:T(8,128)(2,1)S(1)} %collective-permute-done.8), channel_id=1, source_target_pairs={{0,8},{8,16},{16,24},{24,32},{32,40},{40,48},{48,56},{56,64},{64,7... | collective-permute-start | bytes 1572872 | tf_op jit(solution)/shard_map/ppermute | solution.py:28
  23.7 14.6 %copy-start.10 = (bf16[128,2048]{0,1:T(8,128)(2,1)}, bf16[128,2048]{0,1:T(8,128)(2,1)S(1)}, u32[]{:S(2)}) copy-start(bf16[128,2048]{0,1:T(8,128)(2,1)S(1)} %collective-permute-done.1) | copy-start | bytes 1572868
  23.7 11.3 %collective-permute-start.2 = (bf16[128,2048]{0,1:T(8,128)(2,1)S(1)}, bf16[128,2048]{0,1:T(8,128)(2,1)}, u32[]{:S(2)}, u32[]{:S(2)}) collective-permute-start(bf16[128,2048]{0,1:T(8,128)(2,1)S(1)} %collective-permute-done.1), channel_id=1, source_target_pairs={{0,8},{8,16},{16,24},{24,32},{32,40},{40,48},{48,56},{56,64},{64,7... | collective-permute-start | bytes 1572872 | tf_op jit(solution)/shard_map/ppermute | solution.py:28
  29.3 33.1 %copy-start.6 = (bf16[128,2048]{0,1:T(8,128)(2,1)}, bf16[128,2048]{0,1:T(8,128)(2,1)S(1)}, u32[]{:S(2)}) copy-start(bf16[128,2048]{0,1:T(8,128)(2,1)S(1)} %collective-permute-done.9) | copy-start | bytes 1572868
  29.3 14.7 %collective-permute-start.10 = (bf16[128,2048]{0,1:T(8,128)(2,1)S(1)}, bf16[128,2048]{0,1:T(8,128)(2,1)}, u32[]{:S(2)}, u32[]{:S(2)}) collective-permute-start(bf16[128,2048]{0,1:T(8,128)(2,1)S(1)} %collective-permute-done.9), channel_id=1, source_target_pairs={{0,8},{8,16},{16,24},{24,32},{32,40},{40,48},{48,56},{56,64},{64,7... | collective-permute-start | bytes 1572872 | tf_op jit(solution)/shard_map/ppermute | solution.py:28
  35.0 12.3 %collective-permute-start.3 = (bf16[128,2048]{0,1:T(8,128)(2,1)}, bf16[128,2048]{0,1:T(8,128)(2,1)}, u32[]{:S(2)}, u32[]{:S(2)}) collective-permute-start(bf16[128,2048]{0,1:T(8,128)(2,1)} %collective-permute-done.2), channel_id=1, source_target_pairs={{0,8},{8,16},{16,24},{24,32},{32,40},{40,48},{48,56},{56,64},{64,7... | collective-permute-start | bytes 1572872 | tf_op jit(solution)/shard_map/ppermute | solution.py:28
  38.3 24.1 %collective-permute-start.7 = (bf16[128,2048]{0,1:T(8,128)(2,1)S(1)}, bf16[128,2048]{0,1:T(8,128)(2,1)S(1)}, u32[]{:S(2)}, u32[]{:S(2)}) collective-permute-start(bf16[128,2048]{0,1:T(8,128)(2,1)S(1)} %bitcast.92), channel_id=1, source_target_pairs={{0,128},{128,0},{1,129},{129,1},{2,130},{130,2},{3,131},{131,3},{4... | collective-permute-start | bytes 1572872 | tf_op jit(solution)/shard_map/ppermute | solution.py:22
  42.9 23.3 %collective-permute-start.6 = (bf16[128,2048]{0,1:T(8,128)(2,1)S(1)}, bf16[128,2048]{0,1:T(8,128)(2,1)}, u32[]{:S(2)}, u32[]{:S(2)}) collective-permute-start(bf16[128,2048]{0,1:T(8,128)(2,1)S(1)} %bitcast.90), channel_id=1, source_target_pairs={{0,128},{128,0},{1,129},{129,1},{2,130},{130,2},{3,131},{131,3},{4... | collective-permute-start | bytes 1572872 | tf_op jit(solution)/shard_map/ppermute | solution.py:22
  44.0 10.8 %collective-permute-start.11 = (bf16[128,2048]{0,1:T(8,128)(2,1)}, bf16[128,2048]{0,1:T(8,128)(2,1)}, u32[]{:S(2)}, u32[]{:S(2)}) collective-permute-start(bf16[128,2048]{0,1:T(8,128)(2,1)} %collective-permute-done.10), channel_id=1, source_target_pairs={{0,8},{8,16},{16,24},{24,32},{32,40},{40,48},{48,56},{56,64},{64,7... | collective-permute-start | bytes 1572872 | tf_op jit(solution)/shard_map/ppermute | solution.py:28
  47.4 13.0 %collective-permute-start.4 = (bf16[128,2048]{0,1:T(8,128)(2,1)}, bf16[128,2048]{0,1:T(8,128)(2,1)}, u32[]{:S(2)}, u32[]{:S(2)}) collective-permute-start(bf16[128,2048]{0,1:T(8,128)(2,1)} %collective-permute-done.3), channel_id=1, source_target_pairs={{0,8},{8,16},{16,24},{24,32},{32,40},{40,48},{48,56},{56,64},{64,7... | collective-permute-start | bytes 1572872 | tf_op jit(solution)/shard_map/ppermute | solution.py:28
  54.8 14.4 %collective-permute-start.12 = (bf16[128,2048]{0,1:T(8,128)(2,1)}, bf16[128,2048]{0,1:T(8,128)(2,1)}, u32[]{:S(2)}, u32[]{:S(2)}) collective-permute-start(bf16[128,2048]{0,1:T(8,128)(2,1)} %collective-permute-done.11), channel_id=1, source_target_pairs={{0,8},{8,16},{16,24},{24,32},{32,40},{40,48},{48,56},{56,64},{64,7... | collective-permute-start | bytes 1572872 | tf_op jit(solution)/shard_map/ppermute | solution.py:28
  60.4 12.7 %collective-permute-start.5 = (bf16[128,2048]{0,1:T(8,128)(2,1)}, bf16[128,2048]{0,1:T(8,128)(2,1)}, u32[]{:S(2)}, u32[]{:S(2)}) collective-permute-start(bf16[128,2048]{0,1:T(8,128)(2,1)} %collective-permute-done.4), channel_id=1, source_target_pairs={{0,8},{8,16},{16,24},{24,32},{32,40},{40,48},{48,56},{56,64},{64,7... | collective-permute-start | bytes 1572872 | tf_op jit(solution)/shard_map/ppermute | solution.py:28
  62.4 0.8 copy-start.3
  67.8 13.1 %copy-start.11 = (bf16[128,2048]{0,1:T(8,128)(2,1)S(1)}, bf16[128,2048]{0,1:T(8,128)(2,1)}, u32[]{:S(2)}) copy-start(bf16[128,2048]{0,1:T(8,128)(2,1)} %copy-done.10) | copy-start | bytes 1572868
  67.8 14.0 %copy-start.9 = (bf16[128,2048]{0,1:T(8,128)(2,1)S(1)}, bf16[128,2048]{0,1:T(8,128)(2,1)}, u32[]{:S(2)}) copy-start(bf16[128,2048]{0,1:T(8,128)(2,1)} %copy-done.8) | copy-start | bytes 1572868
  69.2 20.5 %collective-permute-start.13 = (bf16[128,2048]{0,1:T(8,128)(2,1)}, bf16[128,2048]{0,1:T(8,128)(2,1)S(1)}, u32[]{:S(2)}, u32[]{:S(2)}) collective-permute-start(bf16[128,2048]{0,1:T(8,128)(2,1)} %collective-permute-done.12), channel_id=1, source_target_pairs={{0,8},{8,16},{16,24},{24,32},{32,40},{40,48},{48,56},{56,64},{64,7... | collective-permute-start | bytes 1572872 | tf_op jit(solution)/shard_map/ppermute | solution.py:28
  89.6 6.7 %copy-start.7 = (bf16[128,2048]{0,1:T(8,128)(2,1)S(1)}, bf16[128,2048]{0,1:T(8,128)(2,1)}, u32[]{:S(2)}) copy-start(bf16[128,2048]{0,1:T(8,128)(2,1)} %copy-done.6) | copy-start | bytes 1572868
  89.6 7.7 %copy-start.5 = (bf16[128,2048]{0,1:T(8,128)(2,1)S(1)}, bf16[128,2048]{0,1:T(8,128)(2,1)}, u32[]{:S(2)}) copy-start(bf16[128,2048]{0,1:T(8,128)(2,1)} %copy-done.4) | copy-start | bytes 1572868
  152.9 8.9 %all-to-all-start.1 = ((f32[2,1,8192]{2,1,0:T(1,128)}), f32[2,1,8192]{2,1,0:T(1,128)S(1)}, u32[]{:S(2)}, u32[]{:S(2)}) async-start(f32[2,1,8192]{2,1,0:T(1,128)} %broadcast_in_dim.129), calls=%async_computation.1 | async-start | bytes 131072 | tf_op jit(solution)/shard_map/all_to_all | solution.py:33
  259.1 21.9 %collective-permute-start.21 = (bf16[128,2048]{1,0:T(8,128)(2,1)}, bf16[128,2048]{1,0:T(8,128)(2,1)}, u32[]{:S(2)}, u32[]{:S(2)}) collective-permute-start(bf16[128,2048]{1,0:T(8,128)(2,1)} %copy.147), channel_id=1, source_target_pairs={{8,0},{16,8},{24,16},{32,24},{40,32},{48,40},{56,48},{64,56},{72,6... | collective-permute-start | bytes 1572872 | tf_op jit(solution)/shard_map/ppermute | solution.py:28
  268.6 16.6 %collective-permute-start.15 = (bf16[128,2048]{1,0:T(8,128)(2,1)}, bf16[128,2048]{1,0:T(8,128)(2,1)}, u32[]{:S(2)}, u32[]{:S(2)}) collective-permute-start(bf16[128,2048]{1,0:T(8,128)(2,1)} %copy.140), channel_id=1, source_target_pairs={{8,0},{16,8},{24,16},{32,24},{40,32},{48,40},{56,48},{64,56},{72,6... | collective-permute-start | bytes 1572872 | tf_op jit(solution)/shard_map/ppermute | solution.py:28
  283.3 10.0 %collective-permute-start.22 = (bf16[128,2048]{1,0:T(8,128)(2,1)}, bf16[128,2048]{1,0:T(8,128)(2,1)}, u32[]{:S(2)}, u32[]{:S(2)}) collective-permute-start(bf16[128,2048]{1,0:T(8,128)(2,1)} %add_convert_fusion.5), channel_id=1, source_target_pairs={{8,0},{16,8},{24,16},{32,24},{40,32},{48,40},{56,48},{64,56},{72,6... | collective-permute-start | bytes 1572872 | tf_op jit(solution)/shard_map/ppermute | solution.py:28
  287.5 10.8 %collective-permute-start.16 = (bf16[128,2048]{1,0:T(8,128)(2,1)}, bf16[128,2048]{1,0:T(8,128)(2,1)}, u32[]{:S(2)}, u32[]{:S(2)}) collective-permute-start(bf16[128,2048]{1,0:T(8,128)(2,1)} %add_convert_fusion.11), channel_id=1, source_target_pairs={{8,0},{16,8},{24,16},{32,24},{40,32},{48,40},{56,48},{64,56},{72,6... | collective-permute-start | bytes 1572872 | tf_op jit(solution)/shard_map/ppermute | solution.py:28
  295.5 12.4 %collective-permute-start.23 = (bf16[128,2048]{1,0:T(8,128)(2,1)}, bf16[128,2048]{1,0:T(8,128)(2,1)}, u32[]{:S(2)}, u32[]{:S(2)}) collective-permute-start(bf16[128,2048]{1,0:T(8,128)(2,1)} %add_convert_fusion.4), channel_id=1, source_target_pairs={{8,0},{16,8},{24,16},{32,24},{40,32},{48,40},{56,48},{64,56},{72,6... | collective-permute-start | bytes 1572872 | tf_op jit(solution)/shard_map/ppermute | solution.py:28
  300.5 11.6 %collective-permute-start.17 = (bf16[128,2048]{1,0:T(8,128)(2,1)}, bf16[128,2048]{1,0:T(8,128)(2,1)}, u32[]{:S(2)}, u32[]{:S(2)}) collective-permute-start(bf16[128,2048]{1,0:T(8,128)(2,1)} %add_convert_fusion.10), channel_id=1, source_target_pairs={{8,0},{16,8},{24,16},{32,24},{40,32},{48,40},{56,48},{64,56},{72,6... | collective-permute-start | bytes 1572872 | tf_op jit(solution)/shard_map/ppermute | solution.py:28
  305.2 11.7 %copy-start = (f32[256,16,128]{0,2,1:T(8,128)S(1)}, f32[256,16,128]{0,2,1:T(8,128)}, u32[]{:S(2)}) copy-start(f32[256,16,128]{0,2,1:T(8,128)} %get-tuple-element.410) | copy-start | bytes 6291460
  310.2 13.0 %collective-permute-start.24 = (bf16[128,2048]{1,0:T(8,128)(2,1)}, bf16[128,2048]{1,0:T(8,128)(2,1)}, u32[]{:S(2)}, u32[]{:S(2)}) collective-permute-start(bf16[128,2048]{1,0:T(8,128)(2,1)} %add_convert_fusion.3), channel_id=1, source_target_pairs={{8,0},{16,8},{24,16},{32,24},{40,32},{48,40},{56,48},{64,56},{72,6... | collective-permute-start | bytes 1572872 | tf_op jit(solution)/shard_map/ppermute | solution.py:28
  314.4 13.0 %collective-permute-start.18 = (bf16[128,2048]{1,0:T(8,128)(2,1)}, bf16[128,2048]{1,0:T(8,128)(2,1)}, u32[]{:S(2)}, u32[]{:S(2)}) collective-permute-start(bf16[128,2048]{1,0:T(8,128)(2,1)} %add_convert_fusion.9), channel_id=1, source_target_pairs={{8,0},{16,8},{24,16},{32,24},{40,32},{48,40},{56,48},{64,56},{72,6... | collective-permute-start | bytes 1572872 | tf_op jit(solution)/shard_map/ppermute | solution.py:28
  325.4 74.1 %collective-permute-start.25 = (bf16[128,2048]{1,0:T(8,128)(2,1)}, bf16[128,2048]{1,0:T(8,128)(2,1)}, u32[]{:S(2)}, u32[]{:S(2)}) collective-permute-start(bf16[128,2048]{1,0:T(8,128)(2,1)} %add_convert_fusion.2), channel_id=1, source_target_pairs={{8,0},{16,8},{24,16},{32,24},{40,32},{48,40},{56,48},{64,56},{72,6... | collective-permute-start | bytes 1572872 | tf_op jit(solution)/shard_map/ppermute | solution.py:28
  329.6 73.3 %collective-permute-start.19 = (bf16[128,2048]{1,0:T(8,128)(2,1)}, bf16[128,2048]{1,0:T(8,128)(2,1)}, u32[]{:S(2)}, u32[]{:S(2)}) collective-permute-start(bf16[128,2048]{1,0:T(8,128)(2,1)} %add_convert_fusion.8), channel_id=1, source_target_pairs={{8,0},{16,8},{24,16},{32,24},{40,32},{48,40},{56,48},{64,56},{72,6... | collective-permute-start | bytes 1572872 | tf_op jit(solution)/shard_map/ppermute | solution.py:28
  332.4 9.0 %copy-start.1 = (f32[128,16,128]{0,2,1:T(8,128)S(1)}, f32[128,16,128]{0,2,1:T(8,128)}, u32[]{:S(2)}) copy-start(f32[128,16,128]{0,2,1:T(8,128)} %get-tuple-element.683) | copy-start | bytes 3145732
  341.2 67.4 %collective-permute-start.14 = (bf16[128,2048]{1,0:T(8,128)(2,1)}, bf16[128,2048]{1,0:T(8,128)(2,1)}, u32[]{:S(2)}, u32[]{:S(2)}) collective-permute-start(bf16[128,2048]{1,0:T(8,128)(2,1)} %copy.139), channel_id=1, source_target_pairs={{0,128},{128,0},{1,129},{129,1},{2,130},{130,2},{3,131},{131,3},{4... | collective-permute-start | bytes 1572872 | tf_op jit(solution)/shard_map/ppermute | solution.py:22
  343.1 67.5 %copy-start.2 = (f32[128,2048]{1,0:T(8,128)S(1)}, f32[128,2048]{1,0:T(8,128)}, u32[]{:S(2)}) copy-start(f32[128,2048]{1,0:T(8,128)} %copy.153) | copy-start | bytes 3145732
  400.9 9.7 %collective-permute-start.26 = (bf16[128,2048]{1,0:T(8,128)(2,1)S(1)}, bf16[128,2048]{1,0:T(8,128)(2,1)S(1)}, u32[]{:S(2)}, u32[]{:S(2)}) collective-permute-start(bf16[128,2048]{1,0:T(8,128)(2,1)S(1)} %add_convert_fusion.1), channel_id=1, source_target_pairs={{8,0},{16,8},{24,16},{32,24},{40,32},{48,40},{56,48},{64,56},{72,6... | collective-permute-start | bytes 1572872 | tf_op jit(solution)/shard_map/ppermute | solution.py:28
  404.3 11.0 %collective-permute-start.20 = (bf16[128,2048]{1,0:T(8,128)(2,1)S(1)}, bf16[128,2048]{1,0:T(8,128)(2,1)S(1)}, u32[]{:S(2)}, u32[]{:S(2)}) collective-permute-start(bf16[128,2048]{1,0:T(8,128)(2,1)S(1)} %add_convert_fusion.7), channel_id=1, source_target_pairs={{8,0},{16,8},{24,16},{32,24},{40,32},{48,40},{56,48},{64,56},{72,6... | collective-permute-start | bytes 1572872 | tf_op jit(solution)/shard_map/ppermute | solution.py:28
where the time goes:
time: 423 us; the launch traced here: 416 us
  matrix products  110 us (26%)
  local copies, waits for them, and re-layouts  96.1 us (23%)
  blocking collectives  66.2 us (16%)
  starting transfers between devices  64.7 us (15%)
  other arithmetic  40.6 us (10%)
  waiting for transfers between devices  36.1 us (9%)
    ppermute x24, starting transfers between devices, from_behind(): lax.ppermute(value, axis, [(source, source + steps) for source in range(f...  57.3 us
    psum x5, blocking collectives, by_axis(): return functools.reduce(lax.psum, axes, array)  56.4 us
    unnamed x48, local copies, waits for them, and re-layouts  39 us
    ppermute x24, waiting for transfers between devices, from_behind(): lax.ppermute(value, axis, [(source, source + steps) for source in range(f...  30.6 us
    dot_general x16, matrix products, local_scores(): jnp.einsum('pgd,sgd->gps', query_part, key_part, preferred_element_type=j...  28.7 us
    slice x8, local copies, waits for them, and re-layouts, value_block(): return value_flat[position * frames:(position + 1) * frames]  19.4 us
    slice x8, local copies, waits for them, and re-layouts, key_block(): return key_flat[position * frames:(position + 1) * frames]  18.5 us
    dot_general x8, matrix products, backward_group_step(): jnp.einsum('gps,pgd->sgd', weight_low, grad_part, preferred_element_type=...  17.7 us
  transfers between devices with their start and end apart: 28, of which 9 were waited for; matrix products, arithmetic and copies ran while one was open for 22% of the time, Pallas kernels for 0%

commit v1 on v0

v1 whole, which is shorter than its diff:
```python
import functools
import math

import jax
import jax.numpy as jnp
from jax import lax
from jax.experimental import pallas as pl
from jax.experimental.pallas import tpu as pltpu
from jax.sharding import PartitionSpec as P

BLOCK = 128
WINDOW = 7
CHIPS = 8
NEG_FILL = -1e30
MESH = pl.DeviceIdType.MESH
NT = (((1,), (1,)), ((), ()))
NN = (((1,), (0,)), ((), ()))
TN = (((0,), (0,)), ((), ()))
BF = jnp.bfloat16
F32 = jnp.float32


def dot(a, b, dims):
    return lax.dot_general(a, b, dims, preferred_element_type=F32)


def kernel(
    heads,
    lengths,
    bias,
    q_hbm,
    k_hbm,
    v_hbm,
    g_hbm,
    dq_hbm,
    dk_hbm,
    dv_hbm,
    bias_out,
    kv,
    qg,
    tri,
    prob,
    wgrad,
    terms,
    side_out,
    side_in,
    chain_out,
    chain_in,
    dq_own,
    dq_send,
    dq_recv,
    dq_stage,
    out_stage,
    stat_out,
    stat_in,
    load_sem,
    hop_s,
    hop_r,
    side_s,
    side_r,
    swap_s,
    swap_r,
    stat_s,
    stat_r,
    term_s,
    term_r,
    chain_s,
    chain_r,
    dq_s,
    dq_r,
    store_sem,
):
    root_scale = 1.0 / math.sqrt(BLOCK)
    chan = lax.axis_index("chan")
    seq = lax.axis_index("seq")
    chip = lax.div(seq, 2)
    core = lax.rem(seq, 2)
    mate = {"seq": seq + 1 - 2 * core}
    partner = {"chan": 1 - chan}
    above = {"seq": lax.rem(seq + 2, 2 * CHIPS)}
    below = {"seq": lax.rem(seq + 2 * CHIPS - 2, 2 * CHIPS)}
    has_above = chip < CHIPS - 1

    def remote(src, dst, send, recv, where):
        return pltpu.make_async_remote_copy(
            src_ref=src, dst_ref=dst, send_sem=send, recv_sem=recv, device_id=where, device_id_type=MESH
        )

    def loads(j):
        cols = pl.ds(pl.multiple_of(j * BLOCK, BLOCK), BLOCK)
        own = pl.ds(0, BLOCK)
        return (
            pltpu.make_async_copy(k_hbm.at[0, 0, :, cols], kv.at[0, j, 0], load_sem.at[0, j]),
            pltpu.make_async_copy(v_hbm.at[0, 0, :, cols], kv.at[0, j, 1], load_sem.at[1, j]),
            pltpu.make_async_copy(q_hbm.at[0, 0, :, cols], qg.at[j, 0, own], load_sem.at[2, j]),
            pltpu.make_async_copy(g_hbm.at[0, 0, :, cols], qg.at[j, 1, own], load_sem.at[3, j]),
        )

    def stores(j):
        cols = pl.ds(pl.multiple_of(j * BLOCK, BLOCK), BLOCK)
        return (
            pltpu.make_async_copy(out_stage.at[j, 0], dk_hbm.at[0, 0, :, cols], store_sem.at[0, j]),
            pltpu.make_async_copy(out_stage.at[j, 1], dv_hbm.at[0, 0, :, cols], store_sem.at[1, j]),
        )

    def store_query(j):
        cols = pl.ds(pl.multiple_of(j * BLOCK, BLOCK), BLOCK)
        return pltpu.make_async_copy(dq_stage.at[j], dq_hbm.at[0, 0, :, cols], store_sem.at[2, j])

    def hop(n, j):
        return remote(kv.at[2 * n - 2, j], kv.at[2 * n, j], hop_s.at[n - 1, j], hop_r.at[n - 1, j], above)

    def side(n, j):
        i = n - core
        return remote(kv.at[2 * n, j], kv.at[2 * i + 1, j], side_s.at[i, j], side_r.at[i, j], mate)

    def side_arrival(i, j):
        return remote(kv.at[2 * i + 1, j], kv.at[2 * i + 1, j], side_s.at[i, j], side_r.at[i, j], mate)

    def swap(j):
        return remote(
            qg.at[j, :, pl.ds(0, BLOCK)], qg.at[j, :, pl.ds(BLOCK, BLOCK)], swap_s.at[j], swap_r.at[j], partner
        )

    def stat(j):
        return remote(stat_out.at[j], stat_in.at[j], stat_s.at[j], stat_r.at[j], partner)

    def term(i, j):
        h = i + 1 - core
        return remote(side_out.at[i, j], side_in.at[h, j], term_s.at[i, j], term_r.at[h, j], mate)

    def term_arrival(h, j):
        return remote(side_in.at[h, j], side_in.at[h, j], term_s.at[0, j], term_r.at[h, j], mate)

    def chain(h, j):
        return remote(
            chain_out.at[h - 1, j], chain_in.at[h - 1, j], chain_s.at[h - 1, j], chain_r.at[h - 1, j], below
        )

    def query(j):
        return remote(dq_send.at[j], dq_recv.at[j], dq_s.at[j], dq_r.at[j], partner)

    def fetch(j, _):
        for copy in loads(j):
            copy.start()
        return 0

    lax.fori_loop(0, heads, fetch, 0)

    barrier = pltpu.get_barrier_semaphore()
    pl.semaphore_signal(barrier, inc=1, device_id=mate, device_id_type=MESH)
    pl.semaphore_signal(barrier, inc=1, device_id=partner, device_id_type=MESH)

    @pl.when(has_above)
    def _():
        pl.semaphore_signal(barrier, inc=1, device_id=above, device_id_type=MESH)

    @pl.when(chip > 0)
    def _():
        pl.semaphore_signal(barrier, inc=1, device_id=below, device_id_type=MESH)

    key_row = lax.broadcasted_iota(jnp.int32, (BLOCK, 2 * BLOCK), 0)
    query_col = lax.rem(lax.broadcasted_iota(jnp.int32, (BLOCK, 2 * BLOCK), 1), BLOCK)
    absent = [jnp.where(seq >= d, 0.0, NEG_FILL).astype(F32) for d in range(WINDOW)]
    tri[0] = jnp.where(key_row <= query_col, 0.0, NEG_FILL)
    tri[1] = jnp.where(key_row > query_col, 0.0, NEG_FILL) + absent[WINDOW - 1]
    lane = lax.rem(lax.broadcasted_iota(jnp.int32, (1, 2 * BLOCK), 1), BLOCK)
    valid = jnp.where(seq * BLOCK + lane < lengths[0], 1.0, 0.0).astype(F32)
    crossed = lax.broadcasted_iota(jnp.int32, (1, 2 * BLOCK), 1) >= BLOCK

    def clear(j, _):
        nothing = jnp.zeros((2, BLOCK, BLOCK), BF)
        for d in range(1, WINDOW):

            @pl.when(seq < d)
            def _():
                kv[d, j] = nothing

        @pl.when(core == 0)
        def _():
            side_in[3, j] = nothing

        @pl.when(core == 1)
        def _():
            side_in[0, j] = nothing

        @pl.when(jnp.logical_not(has_above))
        def _():
            for h in range(3):
                chain_in[h, j] = nothing

        return 0

    lax.fori_loop(0, heads, clear, 0)

    pl.semaphore_wait(barrier, 2 + jnp.where(has_above, 1, 0) + jnp.where(chip > 0, 1, 0))

    def forward(j):
        swap(j).wait_recv()
        for i in range(3):

            @pl.when(seq >= 2 * i + 1)
            def _():
                side_arrival(i, j).wait_recv()

        queries, grads = qg[j, 0], qg[j, 1]
        peak = None
        for d in range(WINDOW):
            score = dot(kv[d, j, 0], queries, NT) * root_scale
            if d == 0:
                score = score + tri[0]
            elif d == WINDOW - 1:
                score = score + tri[1]
            else:
                score = score + absent[d]
            prob[d] = score
            top = jnp.max(score, axis=0, keepdims=True)
            peak = top if peak is None else jnp.maximum(peak, top)
        total = moment = None
        for d in range(WINDOW):
            weight_grad = dot(kv[d, j, 1], grads, NT)
            weight = jnp.exp(prob[d] - peak)
            prob[d] = weight
            wgrad[d] = weight_grad
            a = jnp.sum(weight, axis=0, keepdims=True)
            b = jnp.sum(weight * weight_grad, axis=0, keepdims=True)
            total = a if total is None else total + a
            moment = b if moment is None else moment + b
        offset = jnp.where(crossed, bias[j], 0.0)
        stat_out[j, 0:1] = peak + offset
        stat_out[j, 1:2] = total
        stat_out[j, 2:3] = moment
        stat_out[j, 3:8] = jnp.zeros((5, 2 * BLOCK), F32)
        stat(j).start()

    def backward(j):
        stat(j).wait_recv()

        def turned(row):
            theirs = stat_in[j, row : row + 1]
            return jnp.concatenate([theirs[:, BLOCK:], theirs[:, :BLOCK]], axis=1)

        peak = stat_out[j, 0:1]
        their_peak = turned(0)
        merged = jnp.maximum(peak, their_peak)
        mine, theirs = jnp.exp(peak - merged), jnp.exp(their_peak - merged)
        own_total = stat_out[j, 1:2] * mine
        own_moment = stat_out[j, 2:3] * mine
        inverse = valid / (own_total + turned(1) * theirs)
        delta = (own_moment + turned(2) * theirs) * inverse
        rescale = mine * inverse
        bias_row = (own_moment - delta * own_total) * inverse
        bias_out[pl.ds(j, 1), :] = bias_row[:, BLOCK:]
        queries, grads = qg[j, 0], qg[j, 1]
        query_term = None
        for d in range(WINDOW):
            weight = prob[d] * rescale
            score_grad = (weight * (wgrad[d] - delta)).astype(BF)
            weight = weight.astype(BF)
            value_term = dot(weight, grads, NN)
            key_term = dot(score_grad, queries, NN) * root_scale
            part = dot(score_grad, kv[d, j, 0], TN)
            query_term = part if query_term is None else query_term + part
            if d % 2 == 0:
                terms[d // 2, j, 0] = key_term
                terms[d // 2, j, 1] = value_term
            else:
                side_out[d // 2, j, 0] = key_term.astype(BF)
                side_out[d // 2, j, 1] = value_term.astype(BF)
        query_term = query_term * root_scale
        dq_own[j] = query_term[:BLOCK]
        dq_send[j] = query_term[BLOCK:].astype(BF)
        for i in range(3):

            @pl.when(seq >= 2 * i + 1)
            def _():
                term(i, j).start()

        query(j).start()

    def within(j, action):
        @pl.when(jnp.logical_and(j >= 0, j < heads))
        def _():
            action(j)

    def send_own(j):
        for copy in loads(j):
            copy.wait()

        @pl.when(has_above)
        def _():
            hop(1, j).start()

        @pl.when(core == 0)
        def _():
            side(0, j).start()

        swap(j).start()

    def relay(n, j):
        @pl.when(chip >= n)
        def _():
            hop(n, j).wait_recv()
            if n < 3:

                @pl.when(has_above)
                def _():
                    hop(n + 1, j).start()

                side(n, j).start()
            else:

                @pl.when(core == 1)
                def _():
                    side(n, j).start()

    def finish_query(j):
        query(j).wait_recv()
        dq_stage[j] = (dq_own[j] + dq_recv[j].astype(F32)).astype(BF)
        store_query(j).start()

    def reduce(h, j):
        @pl.when(chip >= h)
        def _():
            if h == 3:
                pl.when(core == 1)(lambda: term_arrival(h, j).wait_recv())
            elif h == 0:
                pl.when(core == 0)(lambda: term_arrival(h, j).wait_recv())
            else:
                term_arrival(h, j).wait_recv()
            total = terms[h, j] + side_in[h, j].astype(F32)
            if h < 3:
                pl.when(has_above)(lambda: chain(h + 1, j).wait_recv())
                total = total + chain_in[h, j].astype(F32)
            if h > 0:
                chain_out[h - 1, j] = total.astype(BF)
                chain(h, j).start()
            else:
                out_stage[j] = total.astype(BF)
                for copy in stores(j):
                    copy.start()

    def step(i, _):
        within(i + 3, send_own)
        within(i + 2, functools.partial(relay, 1))
        within(i + 1, functools.partial(relay, 2))
        within(i, functools.partial(relay, 3))
        within(i - 1, backward)
        within(i, forward)
        within(i - 2, functools.partial(reduce, 3))
        within(i - 3, functools.partial(reduce, 2))
        within(i - 4, functools.partial(reduce, 1))
        within(i - 5, functools.partial(reduce, 0))
        within(i - 2, finish_query)
        return 0

    lax.fori_loop(-3, heads + 5, step, 0)

    def drain(j, _):
        swap(j).wait_send()
        stat(j).wait_send()
        query(j).wait_send()
        store_query(j).wait()
        for copy in stores(j):
            copy.wait()
        for n in range(1, 4):
            pl.when(jnp.logical_and(has_above, chip >= n - 1))(lambda: hop(n, j).wait_send())
        pl.when(core == 0)(lambda: side(0, j).wait_send())
        for n in (1, 2):
            pl.when(chip >= n)(lambda: side(n, j).wait_send())
        pl.when(jnp.logical_and(chip >= 3, core == 1))(lambda: side(3, j).wait_send())
        for i in range(3):
            pl.when(seq >= 2 * i + 1)(lambda: term(i, j).wait_send())
        for h in range(1, 4):
            pl.when(chip >= h)(lambda: chain(h, j).wait_send())
        return 0

    lax.fori_loop(0, heads, drain, 0)


def shards(queries, keys, values, out_grad, cross_bias, lengths):
    heads = cross_bias.shape[0]
    like = jax.ShapeDtypeStruct(queries.shape, BF)
    dma = pltpu.SemaphoreType.DMA
    anywhere = pl.BlockSpec(memory_space=pl.ANY)
    scalar = pl.BlockSpec(memory_space=pltpu.SMEM)
    tile = (BLOCK, BLOCK)
    wide = (BLOCK, 2 * BLOCK)
    query_grad, key_grad, value_grad, bias_rows = pl.pallas_call(
        functools.partial(kernel, heads),
        out_shape=(like, like, like, jax.ShapeDtypeStruct((heads, BLOCK), F32)),
        in_specs=[scalar, scalar] + [anywhere] * 4,
        out_specs=(anywhere, anywhere, anywhere, pl.BlockSpec(memory_space=pltpu.VMEM)),
        scratch_shapes=[
            pltpu.VMEM((WINDOW, heads, 2, *tile), BF),
            pltpu.VMEM((heads, 2, 2 * BLOCK, BLOCK), BF),
            pltpu.VMEM((2, *wide), F32),
            pltpu.VMEM((WINDOW, *wide), F32),
            pltpu.VMEM((WINDOW, *wide), F32),
            pltpu.VMEM((4, heads, 2, *tile), F32),
            pltpu.VMEM((3, heads, 2, *tile), BF),
            pltpu.VMEM((4, heads, 2, *tile), BF),
            pltpu.VMEM((3, heads, 2, *tile), BF),
            pltpu.VMEM((3, heads, 2, *tile), BF),
            pltpu.VMEM((heads, *tile), F32),
            pltpu.VMEM((heads, *tile), BF),
            pltpu.VMEM((heads, *tile), BF),
            pltpu.VMEM((heads, *tile), BF),
            pltpu.VMEM((heads, 2, *tile), BF),
            pltpu.VMEM((heads, 8, 2 * BLOCK), F32),
            pltpu.VMEM((heads, 8, 2 * BLOCK), F32),
            dma((4, heads)),
            dma((3, heads)),
            dma((3, heads)),
            dma((3, heads)),
            dma((3, heads)),
            dma((heads,)),
            dma((heads,)),
            dma((heads,)),
            dma((heads,)),
            dma((3, heads)),
            dma((4, heads)),
            dma((3, heads)),
            dma((3, heads)),
            dma((heads,)),
            dma((heads,)),
            dma((3, heads)),
        ],
        compiler_params=pltpu.CompilerParams(
            collective_id=0, has_side_effects=True, vmem_limit_bytes=56 * 1024 * 1024
        ),
    )(lengths, cross_bias, queries, keys, values, out_grad)
    bias_grad = lax.psum(jnp.sum(bias_rows, axis=1), ("chan", "seq", "dp"))
    return query_grad, key_grad, value_grad, bias_grad


def solution(mesh):
    split = P("dp", "chan", "seq", None)
    return jax.shard_map(
        shards,
        mesh=mesh,
        in_specs=(split, split, split, split, P(), P("dp")),
        out_specs=(split, split, split, P()),
        check_vma=False,
    )
```

time: 423 us -> 201 us (0.48); the launches traced: 416 us -> 199 us
  Pallas kernels: 0 us -> 119 us
  matrix products: 110 us -> 0 us
  local copies, waits for them, and re-layouts: 96.1 us -> 3.97 us
  starting transfers between devices: 64.7 us -> 0 us
  other arithmetic: 40.6 us -> 0.81 us
  waiting for transfers between devices: 36.1 us -> 0 us
  blocking collectives: 66.2 us -> 73.7 us
    pallas_call x0 -> x1, Pallas kernels: none -> 119 us  [shards(): pl.pallas_call(functools.partial(kernel, heads), out_shape=(like, like, l...]
    dot_general x56 -> x0, matrix products: 110 us -> none  [the longest x16 28.7 us: local_scores(): jnp.einsum('pgd,sgd->gps', query_part, key_part, preferred_element_type=j...]
    ppermute x27 -> x0, starting transfers between devices: 61.3 us -> none  [the longest x24 57.3 us: from_behind(): lax.ppermute(value, axis, [(source, source + steps) for source in range(f...]
    slice x19 -> x0, local copies, waits for them, and re-layouts: 37.9 us -> none  [the longest x8 19.4 us: value_block(): return value_flat[position * frames:(position + 1) * frames]]
    unnamed x48 -> x7, local copies, waits for them, and re-layouts: 39 us -> 3.97 us
    ppermute x27 -> x0, waiting for transfers between devices: 30.7 us -> none  [the longest x24 30.6 us: from_behind(): lax.ppermute(value, axis, [(source, source + steps) for source in range(f...]
    convert_element_type x20 -> x0, other arithmetic: 21.9 us -> none  [the longest x5 10.5 us: shards(): running[0].astype(jnp.bfloat16)]
    psum x5 -> x1, blocking collectives: 56.4 us -> 73.7 us  [shards(): bias_grad = lax.psum(jnp.sum(bias_rows, axis=1), ('chan', 'seq', 'dp'))]
  transfers between devices with their start and end apart: 28 -> 0, of which waited for: 9 -> 0; matrix products, arithmetic and copies ran while one was open for 22% -> 0% of each run, Pallas kernels for 0% -> 0%
where the time goes in v1:
time: 201 us; the launch traced here: 199 us
  Pallas kernels  119 us (59%)
  blocking collectives  73.7 us (37%)
  local copies, waits for them, and re-layouts  3.97 us (2%)
    pallas_call x1, Pallas kernels, shards(): pl.pallas_call(functools.partial(kernel, heads), out_shape=(like, like, l...  119 us
    psum x1, blocking collectives, shards(): bias_grad = lax.psum(jnp.sum(bias_rows, axis=1), ('chan', 'seq', 'dp'))  73.7 us

profile of v1, /device:TPU:32, one launch (start us, length us, event | category | flops | bytes accessed | tf_op | source)
XLA Modules:
  0.0 198.8 jit_solution(14488901055310291835)
XLA Ops:
  1.3 119.0 %shard_map.93 = (bf16[1,1,128,2048]{3,2,1,0:T(8,128)(2,1)}, bf16[1,1,128,2048]{3,2,1,0:T(8,128)(2,1)}, bf16[1,1,128,2048]{3,2,1,0:T(8,128)(2,1)}, f32[16,128]{1,0:T(8,128)}) custom-call(s32[1]{0:T(128)S(6)} %copy.13.lengths, f32[16]{0:T(128)} %bias.1, bf16[1,1,128,2048]{3,2,1,0:T(8,128)(2,1)} %q_hbm.1, bf16[1,1,128,2048]{3,2,1,0:T(8,128)(2,1)} %k_hbm.1, ...), custom_call_target="tpu_custom_call" | custom-call | tf_op jit(solution)/shard_map/pallas_call | solution.py:389
  120.3 0.8 reduce_sum.9
  121.1 73.7 %psum.7 = f32[16]{0:T(128)} all-reduce(f32[16]{0:T(128)S(1)} %reduce_sum.9), channel_id=1, replica_groups=mesh['chan'=2,'seq'=16,'dp'=8] {'chan','seq','dp'}, use_global_device_ids=true, to_apply=%region_1.0 | all-reduce | flops 16 | bytes 128 | tf_op jit(solution)/shard_map/psum | solution.py:433
  194.8 0.0 copy-start.1
  194.8 1.9 copy.14
  196.8 0.0 copy-done.1
  196.8 0.0 copy-start
  196.8 0.8 copy.15
  197.6 0.4 copy-done
  198.0 0.8 copy.16
Async XLA Ops:
  194.8 1.9 copy-start.1
  196.8 1.2 copy-start

commit v2 on v1

--- a/solution.py
+++ b/solution.py
@@ -10,7 +10,6 @@
 
 BLOCK = 128
 WINDOW = 7
-CHIPS = 8
 NEG_FILL = -1e30
 MESH = pl.DeviceIdType.MESH
 NT = (((1,), (1,)), ((), ()))
@@ -26,6 +25,8 @@
 
 def kernel(
     heads,
+    chips,
+    convs,
     lengths,
     bias,
     q_hbm,
@@ -53,6 +54,10 @@
     out_stage,
     stat_out,
     stat_in,
+    bias_mate,
+    bias_seq,
+    bias_row,
+    bias_col,
     load_sem,
     hop_s,
     hop_r,
@@ -69,6 +74,13 @@
     dq_s,
     dq_r,
     store_sem,
+    mate_sem,
+    seq_s,
+    seq_r,
+    row_s,
+    row_r,
+    col_s,
+    col_r,
 ):
     root_scale = 1.0 / math.sqrt(BLOCK)
     chan = lax.axis_index("chan")
@@ -77,9 +89,32 @@
     core = lax.rem(seq, 2)
     mate = {"seq": seq + 1 - 2 * core}
     partner = {"chan": 1 - chan}
-    above = {"seq": lax.rem(seq + 2, 2 * CHIPS)}
-    below = {"seq": lax.rem(seq + 2 * CHIPS - 2, 2 * CHIPS)}
-    has_above = chip < CHIPS - 1
+    above = {"seq": lax.rem(seq + 2, 2 * chips)}
+    below = {"seq": lax.rem(seq + 2 * chips - 2, 2 * chips)}
+    has_above = chip < chips - 1
+    conv = lax.axis_index("dp")
+    row = 2 * chan + lax.rem(conv, 2)
+    col = lax.div(conv, 2)
+    rows, cols = (4, convs // 2) if convs > 1 else (2, 1)
+    row_step = 1 if convs > 1 else 2
+
+    def chip_peer(k):
+        there = lax.rem(chip + k, chips)
+        return there, {"seq": 2 * there + core}
+
+    def row_peer(k):
+        there = lax.rem(row + k * row_step, 4)
+        return there, {"chan": lax.div(there, 2), "dp": conv - lax.rem(conv, 2) + lax.rem(there, 2)}
+
+    def col_peer(k):
+        there = lax.rem(col + k, cols)
+        return there, {"dp": 2 * there + lax.rem(conv, 2)}
+
+    groups = (
+        (bias_seq, seq_s, seq_r, chip, chip_peer, chips),
+        (bias_row, row_s, row_r, row, row_peer, rows),
+        (bias_col, col_s, col_r, col, col_peer, cols),
+    )
 
     def remote(src, dst, send, recv, where):
         return pltpu.make_async_remote_copy(
@@ -149,15 +184,9 @@
 
     barrier = pltpu.get_barrier_semaphore()
     pl.semaphore_signal(barrier, inc=1, device_id=mate, device_id_type=MESH)
-    pl.semaphore_signal(barrier, inc=1, device_id=partner, device_id_type=MESH)
-
-    @pl.when(has_above)
-    def _():
-        pl.semaphore_signal(barrier, inc=1, device_id=above, device_id_type=MESH)
-
-    @pl.when(chip > 0)
-    def _():
-        pl.semaphore_signal(barrier, inc=1, device_id=below, device_id_type=MESH)
+    for *_, peer, size in groups:
+        for k in range(1, size):
+            pl.semaphore_signal(barrier, inc=1, device_id=peer(k)[1], device_id_type=MESH)
 
     key_row = lax.broadcasted_iota(jnp.int32, (BLOCK, 2 * BLOCK), 0)
     query_col = lax.rem(lax.broadcasted_iota(jnp.int32, (BLOCK, 2 * BLOCK), 1), BLOCK)
@@ -193,7 +222,7 @@
 
     lax.fori_loop(0, heads, clear, 0)
 
-    pl.semaphore_wait(barrier, 2 + jnp.where(has_above, 1, 0) + jnp.where(chip > 0, 1, 0))
+    pl.semaphore_wait(barrier, chips + rows + cols - 2)
 
     def forward(j):
         swap(j).wait_recv()
@@ -249,8 +278,14 @@
         inverse = valid / (own_total + turned(1) * theirs)
         delta = (own_moment + turned(2) * theirs) * inverse
         rescale = mine * inverse
-        bias_row = (own_moment - delta * own_total) * inverse
-        bias_out[pl.ds(j, 1), :] = bias_row[:, BLOCK:]
+        offset_term = (own_moment - delta * own_total) * inverse
+        bias_out[pl.ds(j, 1), :] = offset_term[:, BLOCK:]
+
+        @pl.when(j == heads - 1)
+        def _():
+            bias_out[...] = jnp.broadcast_to(jnp.sum(bias_out[...], axis=1, keepdims=True), bias_out.shape)
+            mate_total().start()
+
         queries, grads = qg[j, 0], qg[j, 1]
         query_term = None
         for d in range(WINDOW):
@@ -278,6 +313,36 @@
 
         query(j).start()
 
+    def mate_total():
+        return remote(bias_out, bias_mate, mate_sem.at[0], mate_sem.at[1], mate)
+
+    def spread(group):
+        ref, send, recv, mine, peer, size = groups[group]
+        for k in range(1, size):
+            remote(ref.at[mine], ref.at[mine], send.at[k], recv.at[mine], peer(k)[1]).start()
+
+    def gather(group):
+        ref, send, recv, mine, peer, size = groups[group]
+        for k in range(1, size):
+            there, where = peer(k)
+            remote(ref.at[there], ref.at[there], send.at[k], recv.at[there], where).wait_recv()
+        slots = [ref[n * row_step if group == 1 else n] for n in range(size)]
+        return functools.reduce(jnp.add, slots)
+
+    def bias_stage(n):
+        if n == 0:
+            mate_total().wait_recv()
+            bias_seq[chip] = bias_out[...] + bias_mate[...]
+            spread(0)
+        elif n == 1:
+            bias_row[row] = gather(0)
+            spread(1)
+        elif n == 2:
+            bias_col[col] = gather(1)
+            spread(2)
+        else:
+            bias_mate[...] = gather(2)
+
     def within(j, action):
         @pl.when(jnp.logical_and(j >= 0, j < heads))
         def _():
@@ -352,6 +417,8 @@
         within(i - 4, functools.partial(reduce, 1))
         within(i - 5, functools.partial(reduce, 0))
         within(i - 2, finish_query)
+        for n in range(4):
+            pl.when(i == heads + 1 + n)(functools.partial(bias_stage, n))
         return 0
 
     lax.fori_loop(-3, heads + 5, step, 0)
@@ -376,10 +443,16 @@
         return 0
 
     lax.fori_loop(0, heads, drain, 0)
+    mate_total().wait_send()
+    for ref, send, recv, mine, peer, size in groups:
+        for k in range(1, size):
+            remote(ref.at[mine], ref.at[mine], send.at[k], recv.at[mine], peer(k)[1]).wait_send()
+    bias_out[...] = bias_mate[...]
 
 
 def shards(queries, keys, values, out_grad, cross_bias, lengths):
     heads = cross_bias.shape[0]
+    chips, convs = lax.axis_size("seq") // 2, lax.axis_size("dp")
     like = jax.ShapeDtypeStruct(queries.shape, BF)
     dma = pltpu.SemaphoreType.DMA
     anywhere = pl.BlockSpec(memory_space=pl.ANY)
@@ -387,7 +460,7 @@
     tile = (BLOCK, BLOCK)
     wide = (BLOCK, 2 * BLOCK)
     query_grad, key_grad, value_grad, bias_rows = pl.pallas_call(
-        functools.partial(kernel, heads),
+        functools.partial(kernel, heads, chips, convs),
         out_shape=(like, like, like, jax.ShapeDtypeStruct((heads, BLOCK), F32)),
         in_specs=[scalar, scalar] + [anywhere] * 4,
         out_specs=(anywhere, anywhere, anywhere, pl.BlockSpec(memory_space=pltpu.VMEM)),
@@ -409,6 +482,10 @@
             pltpu.VMEM((heads, 2, *tile), BF),
             pltpu.VMEM((heads, 8, 2 * BLOCK), F32),
             pltpu.VMEM((heads, 8, 2 * BLOCK), F32),
+            pltpu.VMEM((heads, BLOCK), F32),
+            pltpu.VMEM((chips, heads, BLOCK), F32),
+            pltpu.VMEM((4, heads, BLOCK), F32),
+            pltpu.VMEM((4, heads, BLOCK), F32),
             dma((4, heads)),
             dma((3, heads)),
             dma((3, heads)),
@@ -425,13 +502,19 @@
             dma((heads,)),
             dma((heads,)),
             dma((3, heads)),
+            dma((2,)),
+            dma((chips,)),
+            dma((chips,)),
+            dma((4,)),
+            dma((4,)),
+            dma((4,)),
+            dma((4,)),
         ],
         compiler_params=pltpu.CompilerParams(
             collective_id=0, has_side_effects=True, vmem_limit_bytes=56 * 1024 * 1024
         ),
     )(lengths, cross_bias, queries, keys, values, out_grad)
-    bias_grad = lax.psum(jnp.sum(bias_rows, axis=1), ("chan", "seq", "dp"))
-    return query_grad, key_grad, value_grad, bias_grad
+    return query_grad, key_grad, value_grad, bias_rows[:, 0]
 
 
 def solution(mesh):

time: 201 us -> 134 us (0.67)
  blocking collectives: 73.7 us -> 0 us
  Pallas kernels: 119 us -> 127 us
    psum x1 -> x0, blocking collectives: 73.7 us -> none  [shards(): bias_grad = lax.psum(jnp.sum(bias_rows, axis=1), ('chan', 'seq', 'dp'))]
    pallas_call x1, Pallas kernels: 119 us -> 127 us  [shards(): pl.pallas_call(functools.partial(kernel, heads, chips, convs), out_shape=...]
where the time goes in v2:
time: 134 us
  Pallas kernels  127 us (95%)
  local copies, waits for them, and re-layouts  5.29 us (4%)
    pallas_call x1, Pallas kernels, shards(): pl.pallas_call(functools.partial(kernel, heads, chips, convs), out_shape=...  127 us
    unnamed x7, local copies, waits for them, and re-layouts  3.96 us

profile of v2, /device:TPU:32, one launch (start us, length us, event | category | flops | bytes accessed | tf_op | source)
XLA Modules:
  0.0 133.6 jit_solution(7652956923952213048)
XLA Ops:
  1.3 127.0 %shard_map.93 = (bf16[1,1,128,2048]{3,2,1,0:T(8,128)(2,1)}, bf16[1,1,128,2048]{3,2,1,0:T(8,128)(2,1)}, bf16[1,1,128,2048]{3,2,1,0:T(8,128)(2,1)}, f32[16,128]{1,0:T(8,128)}) custom-call(s32[1]{0:T(128)S(6)} %copy.13.lengths, f32[16]{0:T(128)} %bias.1, bf16[1,1,128,2048]{3,2,1,0:T(8,128)(2,1)} %q_hbm.1, bf16[1,1,128,2048]{3,2,1,0:T(8,128)(2,1)} %k_hbm.1, ...), custom_call_target="tpu_custom_call" | custom-call | tf_op jit(solution)/shard_map/pallas_call | solution.py:462
  128.3 1.3 slice_reduce_fusion
  129.6 0.0 copy-start.1
  129.6 1.9 %copy.14 = bf16[1,1,128,2048]{3,2,1,0:T(8,128)(2,1)} copy(bf16[1,1,128,2048]{3,2,1,0:T(8,128)(2,1)} %get-tuple-element.16) | data formatting | bytes 1048576
  131.5 0.0 copy-done.1
  131.5 0.0 copy-start
  131.6 0.8 copy.15
  132.3 0.4 copy-done
  132.8 0.8 copy.16
Async XLA Ops:
  129.6 1.9 %copy-start.1 = (bf16[1,1,128,2048]{3,2,1,0:T(8,128)(2,1)S(1)}, bf16[1,1,128,2048]{3,2,1,0:T(8,128)(2,1)}, u32[]{:S(2)}) copy-start(bf16[1,1,128,2048]{3,2,1,0:T(8,128)(2,1)} %get-tuple-element.17) | copy-start | bytes 1572868
  131.5 1.2 copy-start

commit v3 on v2

--- a/solution.py
+++ b/solution.py
@@ -233,6 +233,7 @@
                 side_arrival(i, j).wait_recv()
 
         queries, grads = qg[j, 0], qg[j, 1]
+        slot = lax.rem(j, 2)
         peak = None
         for d in range(WINDOW):
             score = dot(kv[d, j, 0], queries, NT) * root_scale
@@ -242,15 +243,15 @@
                 score = score + tri[1]
             else:
                 score = score + absent[d]
-            prob[d] = score
+            prob[slot, d] = score
             top = jnp.max(score, axis=0, keepdims=True)
             peak = top if peak is None else jnp.maximum(peak, top)
         total = moment = None
         for d in range(WINDOW):
             weight_grad = dot(kv[d, j, 1], grads, NT)
-            weight = jnp.exp(prob[d] - peak)
-            prob[d] = weight
-            wgrad[d] = weight_grad
+            weight = jnp.exp(prob[slot, d] - peak)
+            prob[slot, d] = weight
+            wgrad[slot, d] = weight_grad
             a = jnp.sum(weight, axis=0, keepdims=True)
             b = jnp.sum(weight * weight_grad, axis=0, keepdims=True)
             total = a if total is None else total + a
@@ -287,10 +288,11 @@
             mate_total().start()
 
         queries, grads = qg[j, 0], qg[j, 1]
+        slot = lax.rem(j, 2)
         query_term = None
         for d in range(WINDOW):
-            weight = prob[d] * rescale
-            score_grad = (weight * (wgrad[d] - delta)).astype(BF)
+            weight = prob[slot, d] * rescale
+            score_grad = (weight * (wgrad[slot, d] - delta)).astype(BF)
             weight = weight.astype(BF)
             value_term = dot(weight, grads, NN)
             key_term = dot(score_grad, queries, NN) * root_scale
@@ -406,22 +408,22 @@
                     copy.start()
 
     def step(i, _):
-        within(i + 3, send_own)
         within(i + 2, functools.partial(relay, 1))
         within(i + 1, functools.partial(relay, 2))
+        within(i + 4, send_own)
         within(i, functools.partial(relay, 3))
+        within(i - 4, functools.partial(reduce, 2))
+        within(i - 5, functools.partial(reduce, 1))
+        within(i - 2, functools.partial(reduce, 3))
+        within(i - 6, functools.partial(reduce, 0))
+        within(i, forward)
         within(i - 1, backward)
-        within(i, forward)
-        within(i - 2, functools.partial(reduce, 3))
-        within(i - 3, functools.partial(reduce, 2))
-        within(i - 4, functools.partial(reduce, 1))
-        within(i - 5, functools.partial(reduce, 0))
-        within(i - 2, finish_query)
+        within(i - 3, finish_query)
         for n in range(4):
-            pl.when(i == heads + 1 + n)(functools.partial(bias_stage, n))
+            pl.when(i == heads + 1 + 1 * n)(functools.partial(bias_stage, n))
         return 0
 
-    lax.fori_loop(-3, heads + 5, step, 0)
+    lax.fori_loop(-4, heads + 6, step, 0)
 
     def drain(j, _):
         swap(j).wait_send()
@@ -468,8 +470,8 @@
             pltpu.VMEM((WINDOW, heads, 2, *tile), BF),
             pltpu.VMEM((heads, 2, 2 * BLOCK, BLOCK), BF),
             pltpu.VMEM((2, *wide), F32),
-            pltpu.VMEM((WINDOW, *wide), F32),
-            pltpu.VMEM((WINDOW, *wide), F32),
+            pltpu.VMEM((2, WINDOW, *wide), F32),
+            pltpu.VMEM((2, WINDOW, *wide), F32),
             pltpu.VMEM((4, heads, 2, *tile), F32),
             pltpu.VMEM((3, heads, 2, *tile), BF),
             pltpu.VMEM((4, heads, 2, *tile), BF),

time: 134 us -> 124 us (0.925)
  Pallas kernels: 127 us -> 117 us
    pallas_call x1, Pallas kernels: 127 us -> 117 us  [shards(): pl.pallas_call(functools.partial(kernel, heads, chips, convs), out_shape=...]
where the time goes in v3:
time: 124 us; the launch traced here: 123 us
  Pallas kernels  117 us (94%)
  local copies, waits for them, and re-layouts  5.29 us (4%)
  between operations  1.29 us (1%)
    pallas_call x1, Pallas kernels, shards(): pl.pallas_call(functools.partial(kernel, heads, chips, convs), out_shape=...  117 us
    unnamed x7, local copies, waits for them, and re-layouts  3.96 us

profile of v3, /device:TPU:32, one launch (start us, length us, event | category | flops | bytes accessed | tf_op | source)
XLA Modules:
  0.0 123.4 jit_solution(10340722752501301059)
XLA Ops:
  1.3 116.8 %shard_map.93 = (bf16[1,1,128,2048]{3,2,1,0:T(8,128)(2,1)}, bf16[1,1,128,2048]{3,2,1,0:T(8,128)(2,1)}, bf16[1,1,128,2048]{3,2,1,0:T(8,128)(2,1)}, f32[16,128]{1,0:T(8,128)}) custom-call(s32[1]{0:T(128)S(6)} %copy.13.lengths, f32[16]{0:T(128)} %bias.1, bf16[1,1,128,2048]{3,2,1,0:T(8,128)(2,1)} %q_hbm.1, bf16[1,1,128,2048]{3,2,1,0:T(8,128)(2,1)} %k_hbm.1, ...), custom_call_target="tpu_custom_call" | custom-call | tf_op jit(solution)/shard_map/pallas_call | solution.py:464
  118.1 1.3 %slice_reduce_fusion = f32[16]{0:T(128)} fusion(f32[16,128]{1,0:T(8,128)} %get-tuple-element.11), kind=kLoop, calls=%fused_computation | loop fusion | bytes 128 | tf_op jit(solution)/shard_map/slice | solution.py:519
  119.5 0.0 copy-start.1
  119.5 1.9 %copy.14 = bf16[1,1,128,2048]{3,2,1,0:T(8,128)(2,1)} copy(bf16[1,1,128,2048]{3,2,1,0:T(8,128)(2,1)} %get-tuple-element.16) | data formatting | bytes 1048576
  121.4 0.0 copy-done.1
  121.4 0.0 copy-start
  121.4 0.8 copy.15
  122.2 0.4 copy-done
  122.6 0.8 copy.16
Async XLA Ops:
  119.5 1.9 %copy-start.1 = (bf16[1,1,128,2048]{3,2,1,0:T(8,128)(2,1)S(1)}, bf16[1,1,128,2048]{3,2,1,0:T(8,128)(2,1)}, u32[]{:S(2)}) copy-start(bf16[1,1,128,2048]{3,2,1,0:T(8,128)(2,1)} %get-tuple-element.17) | copy-start | bytes 1572868
  121.4 1.2 copy-start

commit v4 on v3

--- a/solution.py
+++ b/solution.py
@@ -33,10 +33,9 @@
     k_hbm,
     v_hbm,
     g_hbm,
-    dq_hbm,
-    dk_hbm,
-    dv_hbm,
-    bias_out,
+    dq_stage,
+    out_stage,
+    bias_final,
     kv,
     qg,
     tri,
@@ -50,10 +49,9 @@
     dq_own,
     dq_send,
     dq_recv,
-    dq_stage,
-    out_stage,
     stat_out,
     stat_in,
+    bias_out,
     bias_mate,
     bias_seq,
     bias_row,
@@ -73,7 +71,6 @@
     chain_r,
     dq_s,
     dq_r,
-    store_sem,
     mate_sem,
     seq_s,
     seq_r,
@@ -130,17 +127,6 @@
             pltpu.make_async_copy(q_hbm.at[0, 0, :, cols], qg.at[j, 0, own], load_sem.at[2, j]),
             pltpu.make_async_copy(g_hbm.at[0, 0, :, cols], qg.at[j, 1, own], load_sem.at[3, j]),
         )
-
-    def stores(j):
-        cols = pl.ds(pl.multiple_of(j * BLOCK, BLOCK), BLOCK)
-        return (
-            pltpu.make_async_copy(out_stage.at[j, 0], dk_hbm.at[0, 0, :, cols], store_sem.at[0, j]),
-            pltpu.make_async_copy(out_stage.at[j, 1], dv_hbm.at[0, 0, :, cols], store_sem.at[1, j]),
-        )
-
-    def store_query(j):
-        cols = pl.ds(pl.multiple_of(j * BLOCK, BLOCK), BLOCK)
-        return pltpu.make_async_copy(dq_stage.at[j], dq_hbm.at[0, 0, :, cols], store_sem.at[2, j])
 
     def hop(n, j):
         return remote(kv.at[2 * n - 2, j], kv.at[2 * n, j], hop_s.at[n - 1, j], hop_r.at[n - 1, j], above)
@@ -384,7 +370,6 @@
     def finish_query(j):
         query(j).wait_recv()
         dq_stage[j] = (dq_own[j] + dq_recv[j].astype(F32)).astype(BF)
-        store_query(j).start()
 
     def reduce(h, j):
         @pl.when(chip >= h)
@@ -404,8 +389,6 @@
                 chain(h, j).start()
             else:
                 out_stage[j] = total.astype(BF)
-                for copy in stores(j):
-                    copy.start()
 
     def step(i, _):
         within(i + 2, functools.partial(relay, 1))
@@ -429,9 +412,6 @@
         swap(j).wait_send()
         stat(j).wait_send()
         query(j).wait_send()
-        store_query(j).wait()
-        for copy in stores(j):
-            copy.wait()
         for n in range(1, 4):
             pl.when(jnp.logical_and(has_above, chip >= n - 1))(lambda: hop(n, j).wait_send())
         pl.when(core == 0)(lambda: side(0, j).wait_send())
@@ -449,7 +429,28 @@
     for ref, send, recv, mine, peer, size in groups:
         for k in range(1, size):
             remote(ref.at[mine], ref.at[mine], send.at[k], recv.at[mine], peer(k)[1]).wait_send()
-    bias_out[...] = bias_mate[...]
+    head_row = lax.broadcasted_iota(jnp.int32, (heads, BLOCK), 0)
+    head_lane = lax.broadcasted_iota(jnp.int32, (heads, BLOCK), 1)
+    picked = jnp.where(head_row == head_lane, bias_mate[...], 0.0)
+    bias_final[...] = jnp.sum(picked, axis=0, keepdims=True)
+
+
+def publish(heads, dq_stage, out_stage, bias_final, dq_hbm, dk_hbm, dv_hbm, bias_out, sem):
+    def copies(j):
+        cols = pl.ds(pl.multiple_of(j * BLOCK, BLOCK), BLOCK)
+        return (
+            pltpu.make_async_copy(dq_stage.at[j], dq_hbm.at[0, 0, :, cols], sem.at[0, j]),
+            pltpu.make_async_copy(out_stage.at[j, 0], dk_hbm.at[0, 0, :, cols], sem.at[1, j]),
+            pltpu.make_async_copy(out_stage.at[j, 1], dv_hbm.at[0, 0, :, cols], sem.at[2, j]),
+        )
+
+    for j in range(heads):
+        for copy in copies(j):
+            copy.start()
+    bias_out[...] = bias_final[0, :heads]
+    for j in range(heads):
+        for copy in copies(j):
+            copy.wait()
 
 
 def shards(queries, keys, values, out_grad, cross_bias, lengths):
@@ -461,11 +462,16 @@
     scalar = pl.BlockSpec(memory_space=pltpu.SMEM)
     tile = (BLOCK, BLOCK)
     wide = (BLOCK, 2 * BLOCK)
-    query_grad, key_grad, value_grad, bias_rows = pl.pallas_call(
+    vmem = pl.BlockSpec(memory_space=pltpu.VMEM)
+    staged = pl.pallas_call(
         functools.partial(kernel, heads, chips, convs),
-        out_shape=(like, like, like, jax.ShapeDtypeStruct((heads, BLOCK), F32)),
+        out_shape=(
+            pltpu.VMEM((heads, *tile), BF),
+            pltpu.VMEM((heads, 2, *tile), BF),
+            pltpu.VMEM((1, BLOCK), F32),
+        ),
         in_specs=[scalar, scalar] + [anywhere] * 4,
-        out_specs=(anywhere, anywhere, anywhere, pl.BlockSpec(memory_space=pltpu.VMEM)),
+        out_specs=(vmem, vmem, vmem),
         scratch_shapes=[
             pltpu.VMEM((WINDOW, heads, 2, *tile), BF),
             pltpu.VMEM((heads, 2, 2 * BLOCK, BLOCK), BF),
@@ -480,10 +486,9 @@
             pltpu.VMEM((heads, *tile), F32),
             pltpu.VMEM((heads, *tile), BF),
             pltpu.VMEM((heads, *tile), BF),
-            pltpu.VMEM((heads, *tile), BF),
-            pltpu.VMEM((heads, 2, *tile), BF),
             pltpu.VMEM((heads, 8, 2 * BLOCK), F32),
             pltpu.VMEM((heads, 8, 2 * BLOCK), F32),
+            pltpu.VMEM((heads, BLOCK), F32),
             pltpu.VMEM((heads, BLOCK), F32),
             pltpu.VMEM((chips, heads, BLOCK), F32),
             pltpu.VMEM((4, heads, BLOCK), F32),
@@ -503,7 +508,6 @@
             dma((3, heads)),
             dma((heads,)),
             dma((heads,)),
-            dma((3, heads)),
             dma((2,)),
             dma((chips,)),
             dma((chips,)),
@@ -516,7 +520,14 @@
             collective_id=0, has_side_effects=True, vmem_limit_bytes=56 * 1024 * 1024
         ),
     )(lengths, cross_bias, queries, keys, values, out_grad)
-    return query_grad, key_grad, value_grad, bias_rows[:, 0]
+    return pl.pallas_call(
+        functools.partial(publish, heads),
+        out_shape=(like, like, like, jax.ShapeDtypeStruct((heads,), F32)),
+        in_specs=[vmem, vmem, vmem],
+        out_specs=(anywhere, anywhere, anywhere, vmem),
+        scratch_shapes=[dma((3, heads))],
+        compiler_params=pltpu.CompilerParams(vmem_limit_bytes=4 * 1024 * 1024),
+    )(*staged)
 
 
 def solution(mesh):

time: 124 us -> 119 us (0.960)
  local copies, waits for them, and re-layouts: 5.29 us -> 0 us
    unnamed x7 -> x0, local copies, waits for them, and re-layouts: 3.96 us -> none
    pallas_call x0 -> x1, Pallas kernels: none -> 2.05 us  [shards(): pl.pallas_call(functools.partial(publish, heads), out_shape=(like, like,...]
    slice x1 -> x0, local copies, waits for them, and re-layouts: 1.32 us -> none  [shards(): return (query_grad, key_grad, value_grad, bias_rows[:, 0])]
where the time goes in v4:
time: 119 us
  Pallas kernels  118 us (99%)
  between operations  1.29 us (1%)
    pallas_call x1, Pallas kernels, shards(): pl.pallas_call(functools.partial(kernel, heads, chips, convs), out_shape=...  116 us

profile of v4, /device:TPU:32, one launch (start us, length us, event | category | flops | bytes accessed | tf_op | source)
XLA Modules:
  0.0 119.1 jit_solution(8071128543343288423)
XLA Ops:
  1.3 115.8 %shard_map.93 = (bf16[16,128,128]{2,1,0:T(8,128)(2,1)S(1)}, bf16[16,2,128,128]{3,2,1,0:T(8,128)(2,1)S(1)}, f32[1,128]{1,0:T(1,128)S(1)}) custom-call(s32[1]{0:T(128)S(6)} %copy.10.lengths, f32[16]{0:T(128)} %bias.1, bf16[1,1,128,2048]{3,2,1,0:T(8,128)(2,1)} %q_hbm.1, bf16[1,1,128,2048]{3,2,1,0:T(8,128)(2,1)} %k_hbm.1, bf16[1,1,128,2048]{3,2,1,0:T(8,128)(2,1)} %v_hbm.1, ...), custom_call_target="tpu_custom_call" | custom-call | tf_op jit(solution)/shard_map/pallas_call | solution.py:466
  117.1 2.1 %shard_map.94 = (bf16[1,1,128,2048]{3,2,1,0:T(8,128)(2,1)}, bf16[1,1,128,2048]{3,2,1,0:T(8,128)(2,1)}, bf16[1,1,128,2048]{3,2,1,0:T(8,128)(2,1)}, f32[16]{0:T(128)}) custom-call(bf16[16,128,128]{2,1,0:T(8,128)(2,1)S(1)} %get-tuple-element.7.dq_stage, bf16[16,2,128,128]{3,2,1,0:T(8,128)(2,1)S(1)} %get-tuple-element.8.out_stage, ...), custom_call_target="tpu_custom_call" | custom-call | tf_op jit(solution)/shard_map/pallas_call | solution.py:523

commit v5 on v4

--- a/solution.py
+++ b/solution.py
@@ -54,8 +54,7 @@
     bias_out,
     bias_mate,
     bias_seq,
-    bias_row,
-    bias_col,
+    bias_place,
     load_sem,
     hop_s,
     hop_r,
@@ -74,10 +73,8 @@
     mate_sem,
     seq_s,
     seq_r,
-    row_s,
-    row_r,
-    col_s,
-    col_r,
+    place_s,
+    place_r,
 ):
     root_scale = 1.0 / math.sqrt(BLOCK)
     chan = lax.axis_index("chan")
@@ -90,27 +87,20 @@
     below = {"seq": lax.rem(seq + 2 * chips - 2, 2 * chips)}
     has_above = chip < chips - 1
     conv = lax.axis_index("dp")
-    row = 2 * chan + lax.rem(conv, 2)
-    col = lax.div(conv, 2)
-    rows, cols = (4, convs // 2) if convs > 1 else (2, 1)
-    row_step = 1 if convs > 1 else 2
+    place = chan * convs + conv
+    places = 2 * convs
 
     def chip_peer(k):
         there = lax.rem(chip + k, chips)
         return there, {"seq": 2 * there + core}
 
-    def row_peer(k):
-        there = lax.rem(row + k * row_step, 4)
-        return there, {"chan": lax.div(there, 2), "dp": conv - lax.rem(conv, 2) + lax.rem(there, 2)}
-
-    def col_peer(k):
-        there = lax.rem(col + k, cols)
-        return there, {"dp": 2 * there + lax.rem(conv, 2)}
+    def place_peer(k):
+        there = lax.rem(place + k, places)
+        return there, {"chan": lax.div(there, convs), "dp": lax.rem(there, convs)}
 
     groups = (
         (bias_seq, seq_s, seq_r, chip, chip_peer, chips),
-        (bias_row, row_s, row_r, row, row_peer, rows),
-        (bias_col, col_s, col_r, col, col_peer, cols),
+        (bias_place, place_s, place_r, place, place_peer, places),
     )
 
     def remote(src, dst, send, recv, where):
@@ -208,7 +198,7 @@
 
     lax.fori_loop(0, heads, clear, 0)
 
-    pl.semaphore_wait(barrier, chips + rows + cols - 2)
+    pl.semaphore_wait(barrier, chips + places - 1)
 
     def forward(j):
         swap(j).wait_recv()
@@ -314,8 +304,7 @@
         for k in range(1, size):
             there, where = peer(k)
             remote(ref.at[there], ref.at[there], send.at[k], recv.at[there], where).wait_recv()
-        slots = [ref[n * row_step if group == 1 else n] for n in range(size)]
-        return functools.reduce(jnp.add, slots)
+        return functools.reduce(jnp.add, [ref[n] for n in range(size)])
 
     def bias_stage(n):
         if n == 0:
@@ -323,13 +312,10 @@
             bias_seq[chip] = bias_out[...] + bias_mate[...]
             spread(0)
         elif n == 1:
-            bias_row[row] = gather(0)
+            bias_place[place] = gather(0)
             spread(1)
-        elif n == 2:
-            bias_col[col] = gather(1)
-            spread(2)
         else:
-            bias_mate[...] = gather(2)
+            bias_mate[...] = gather(1)
 
     def within(j, action):
         @pl.when(jnp.logical_and(j >= 0, j < heads))
@@ -402,8 +388,8 @@
         within(i, forward)
         within(i - 1, backward)
         within(i - 3, finish_query)
-        for n in range(4):
-            pl.when(i == heads + 1 + 1 * n)(functools.partial(bias_stage, n))
+        for n in range(3):
+            pl.when(i == heads + 1 + n)(functools.partial(bias_stage, n))
         return 0
 
     lax.fori_loop(-4, heads + 6, step, 0)
@@ -491,8 +477,7 @@
             pltpu.VMEM((heads, BLOCK), F32),
             pltpu.VMEM((heads, BLOCK), F32),
             pltpu.VMEM((chips, heads, BLOCK), F32),
-            pltpu.VMEM((4, heads, BLOCK), F32),
-            pltpu.VMEM((4, heads, BLOCK), F32),
+            pltpu.VMEM((2 * convs, heads, BLOCK), F32),
             dma((4, heads)),
             dma((3, heads)),
             dma((3, heads)),
@@ -511,10 +496,8 @@
             dma((2,)),
             dma((chips,)),
             dma((chips,)),
-            dma((4,)),
-            dma((4,)),
-            dma((4,)),
-            dma((4,)),
+            dma((2 * convs,)),
+            dma((2 * convs,)),
         ],
         compiler_params=pltpu.CompilerParams(
             collective_id=0, has_side_effects=True, vmem_limit_bytes=56 * 1024 * 1024

time: 119 us -> 121 us (1.017)
  no operation moved by 1% of the time
where the time goes in v5:
time: 121 us; the launch traced here: 120 us
  Pallas kernels  119 us (98%)
  between operations  1.29 us (1%)
    pallas_call x1, Pallas kernels, shards(): pl.pallas_call(functools.partial(kernel, heads, chips, convs), out_shape=...  117 us

profile of v5, /device:TPU:32, one launch (start us, length us, event | category | flops | bytes accessed | tf_op | source)
XLA Modules:
  0.0 120.2 jit_solution(11382353647280385761)
XLA Ops:
  1.3 116.9 %shard_map.93 = (bf16[16,128,128]{2,1,0:T(8,128)(2,1)S(1)}, bf16[16,2,128,128]{3,2,1,0:T(8,128)(2,1)S(1)}, f32[1,128]{1,0:T(1,128)S(1)}) custom-call(s32[1]{0:T(128)S(6)} %copy.10.lengths, f32[16]{0:T(128)} %bias.1, bf16[1,1,128,2048]{3,2,1,0:T(8,128)(2,1)} %q_hbm.1, bf16[1,1,128,2048]{3,2,1,0:T(8,128)(2,1)} %k_hbm.1, bf16[1,1,128,2048]{3,2,1,0:T(8,128)(2,1)} %v_hbm.1, ...), custom_call_target="tpu_custom_call" | custom-call | tf_op jit(solution)/shard_map/pallas_call | solution.py:452
  118.2 2.1 %shard_map.94 = (bf16[1,1,128,2048]{3,2,1,0:T(8,128)(2,1)}, bf16[1,1,128,2048]{3,2,1,0:T(8,128)(2,1)}, bf16[1,1,128,2048]{3,2,1,0:T(8,128)(2,1)}, f32[16]{0:T(128)}) custom-call(bf16[16,128,128]{2,1,0:T(8,128)(2,1)S(1)} %get-tuple-element.7.dq_stage, bf16[16,2,128,128]{3,2,1,0:T(8,128)(2,1)S(1)} %get-tuple-element.8.out_stage, ...), custom_call_target="tpu_custom_call" | custom-call | tf_op jit(solution)/shard_map/pallas_call | solution.py:506
